TPU v7x, 32 devices: a whole 2x2x4 slice. The times are simulated.
32 devices in a mesh: dp: 8 (over z, x), ctx: 4 (over y, core).
Axes of the slice: x: 2, y: 2, z: 4, core: 2. Of those that a mesh axis runs over, the one named last changes fastest.
Arguments:
- tokens: bfloat16 [8192, 1536], P(('dp', 'ctx')), may hold values from -6 to 6
- norm_attn: float32 [1536], P(('dp', 'ctx')), may hold values from 0.5 to 1.5
- w_qkv: bfloat16 [3072, 1536], P(('dp', 'ctx')), may hold values from -1 to 1
- w_out: bfloat16 [1536, 1536], P(('dp', 'ctx')), may hold values from -0.875 to 0.875
- norm_mlp: float32 [1536], P(('dp', 'ctx')), may hold values from 0.5 to 1.5
- w_gate_up: bfloat16 [8192, 1536], P(('dp', 'ctx')), may hold values from -0.15625 to 0.15625
- w_down: bfloat16 [1536, 4096], P(('dp', 'ctx')), may hold values from -0.09375 to 0.09375
- cotangent: bfloat16 [8192, 1536], P(('dp', 'ctx')), may hold values from -6 to 6
- seq_lengths: int32 [8, 2], P('dp'), may hold values from 1 to 768, 1024 in all within a row
- block_slot: int32 [8, 8], P('dp'), may hold values from 0 to 7, each once within a row
Outputs:
- result: bfloat16 [8192, 1536], P(('dp', 'ctx'))
- grad_input: float32 [8192, 1536], P(('dp', 'ctx'))
- grad_norm_attn: float32 [1536], P(('dp', 'ctx'))
- grad_qkv: float32 [3072, 1536], P(('dp', 'ctx'))
- grad_out: float32 [1536, 1536], P(('dp', 'ctx'))
- grad_norm_mlp: float32 [1536], P(('dp', 'ctx'))
- grad_gate_up: float32 [8192, 1536], P(('dp', 'ctx'))
- grad_down: float32 [1536, 4096], P(('dp', 'ctx'))
Inputs may be any that keep to these rules, and one draw needn't show every extreme that they name: `seq_lengths`: each row sums to 1024. `block_slot`: each row names every number once; ctx device c of group g holds the blocks of positions c * 2 to (c + 1) * 2 - 1 of that row.
All inputs are finite; a program needn't handle non-finite values.
Results may differ from a plain program's by a relative error of at most 0.025.
Values may be sent and summed in bfloat16 or wider, within the bound.
A program may use at most 320 MiB of HBM per device.

v0:
```python
import math
import jax
import jax.numpy as jnp
from jax import lax
from jax.sharding import PartitionSpec as P

QUERY_HEADS = 16
KEY_VALUE_HEADS = 8
HEAD_SIZE = 96
FF = 4096
BLK = 128
QUERY_FEATURES = 1536
KEY_FEATURES = 768
EPSILON = 1e-05
THETA = 100000.0
MASK_FILL = -1e30


def rope_tables(rope_pos):
    half_dim = HEAD_SIZE // 2
    exponent = jnp.arange(half_dim, dtype=jnp.float32) * (2.0 / HEAD_SIZE)
    frequency = jnp.power(jnp.float32(THETA), -exponent)
    angles = rope_pos.astype(jnp.float32)[:, None] * frequency[None, :]
    return (jnp.cos(angles)[:, None, :], jnp.sin(angles)[:, None, :])


def apply_rotation(values, cosine_table, sine_values):
    half_dim = HEAD_SIZE // 2
    first_half = values[..., :half_dim]
    second_half = values[..., half_dim:]
    return jnp.concatenate(
        [
            first_half * cosine_table - second_half * sine_values,
            second_half * cosine_table + first_half * sine_values,
        ],
        -1,
    )


def rotate_back(gradient, cosine_table, sine_values):
    half_dim = HEAD_SIZE // 2
    first_half = gradient[..., :half_dim]
    second_half = gradient[..., half_dim:]
    return jnp.concatenate(
        [
            first_half * cosine_table + second_half * sine_values,
            second_half * cosine_table - first_half * sine_values,
        ],
        -1,
    )


def positions(lengths, slot_table, first_row, count_of_rows):
    row_index = first_row + jnp.arange(count_of_rows, dtype=jnp.int32)
    block_index = row_index // BLK
    lookup = jnp.arange(slot_table.shape[0], dtype=jnp.int32)
    slot_of = jnp.sum(jnp.where(block_index[:, None] == lookup[None, :], slot_table[None, :], 0), 1)
    stream = slot_of * BLK + row_index % BLK
    seq_ends = jnp.cumsum(lengths)
    passed = stream[:, None] >= seq_ends[None, :]
    segment = jnp.sum(passed.astype(jnp.int32), 1)
    offset = jnp.sum(jnp.where(passed, seq_ends[None, :], 0), 1)
    return (stream, segment, stream - offset)


def norm_back(grad_normed, gain, source, scale):
    weighted = grad_normed * gain
    return scale * weighted - source * scale**3 * jnp.mean(weighted * source, -1, keepdims=True)


def full_product(left_side, whole_weight):
    return jnp.dot(left_side, whole_weight.T, preferred_element_type=jnp.float32)


def full_back(grad_side, whole_weight):
    return jnp.dot(grad_side, whole_weight, preferred_element_type=jnp.float32)


def owned_three(first_part, second_part, third_part):
    return (
        lax.psum_scatter(first_part, ("dp", "ctx"), scatter_dimension=0, tiled=True),
        lax.psum_scatter(second_part, ("dp", "ctx"), scatter_dimension=0, tiled=True),
        lax.psum_scatter(third_part, ("dp", "ctx"), scatter_dimension=0, tiled=True),
    )


def shards(
    tokens, norm_attn, w_qkv, w_out, norm_mlp, w_gate_up, w_down, cotangent, seq_lengths, block_slot
):
    count_of_rows = tokens.shape[0]
    ctx_place = lax.axis_index("ctx")
    lengths = seq_lengths[0]
    slot_table = block_slot[0]
    heads_ratio = QUERY_HEADS // KEY_VALUE_HEADS
    score_scale = 1.0 / math.sqrt(HEAD_SIZE)
    stream, segment, rope_pos = positions(
        lengths, slot_table, ctx_place * count_of_rows, count_of_rows
    )
    cosine_table, sine_values = rope_tables(rope_pos)
    gain_one, gain_two = (
        lax.all_gather(norm_attn, ("dp", "ctx"), axis=0, tiled=True),
        lax.all_gather(norm_mlp, ("dp", "ctx"), axis=0, tiled=True),
    )
    qkv_full, out_full = (
        lax.all_gather(w_qkv, ("dp", "ctx"), axis=0, tiled=True),
        lax.all_gather(w_out, ("dp", "ctx"), axis=0, tiled=True),
    )
    source = tokens.astype(jnp.float32)
    scale_one = lax.rsqrt(jnp.mean(source * source, -1, keepdims=True) + EPSILON)
    normed_one = (source * scale_one * gain_one).astype(jnp.bfloat16)
    projected_output = full_product(normed_one, qkv_full)
    query_rows = apply_rotation(
        projected_output[:, :QUERY_FEATURES].reshape(count_of_rows, QUERY_HEADS, HEAD_SIZE),
        cosine_table,
        sine_values,
    ).astype(jnp.bfloat16)
    keys_mine = apply_rotation(
        projected_output[:, QUERY_FEATURES : QUERY_FEATURES + KEY_FEATURES].reshape(
            count_of_rows, KEY_VALUE_HEADS, HEAD_SIZE
        ),
        cosine_table,
        sine_values,
    ).astype(jnp.bfloat16)
    values_mine = projected_output[:, QUERY_FEATURES + KEY_FEATURES :].astype(jnp.bfloat16)
    grouped_queries = query_rows.reshape(count_of_rows, KEY_VALUE_HEADS, heads_ratio, HEAD_SIZE)
    key_value = jnp.concatenate([keys_mine.reshape(count_of_rows, KEY_FEATURES), values_mine], 1)

    def masked(block_portion, start_row):
        portion_rows = block_portion.shape[0]
        key_stream, key_segment, unused = positions(lengths, slot_table, start_row, portion_rows)
        key_portion = block_portion[:, :KEY_FEATURES].reshape(
            portion_rows, KEY_VALUE_HEADS, HEAD_SIZE
        )
        value_portion = block_portion[:, KEY_FEATURES:].reshape(
            portion_rows, KEY_VALUE_HEADS, HEAD_SIZE
        )
        scores = (
            jnp.einsum(
                "rgjd,ngd->gjrn", grouped_queries, key_portion, preferred_element_type=jnp.float32
            )
            * score_scale
        )
        allowed = (
            (segment[:, None] == key_segment[None, :]) & (key_stream[None, :] <= stream[:, None])
        )[None, None]
        return (jnp.where(allowed, scores, MASK_FILL), allowed, key_portion, value_portion)

    highest_score = jnp.full((KEY_VALUE_HEADS, heads_ratio, count_of_rows), MASK_FILL, jnp.float32)
    scores, allowed, key_portion, value_portion = masked(
        lax.all_gather(key_value, "ctx", axis=0, tiled=True), jnp.int32(0)
    )
    new_high = jnp.maximum(highest_score, jnp.max(scores, -1))
    weights = jnp.where(allowed, jnp.exp(scores - new_high[..., None]), 0.0)
    weight_sum = jnp.sum(weights, -1)
    gained = jnp.einsum(
        "gjrn,ngd->rgjd",
        weights.astype(jnp.bfloat16),
        value_portion,
        preferred_element_type=jnp.float32,
    )
    accumulated = gained
    highest_score, weight_sum, accumulated = (new_high, weight_sum, accumulated)
    log_total = highest_score + jnp.log(weight_sum)
    attention_output = (
        (accumulated / jnp.transpose(weight_sum, (2, 0, 1))[..., None])
        .astype(jnp.bfloat16)
        .reshape(count_of_rows, QUERY_FEATURES)
    )
    residual = source + full_product(attention_output, out_full)
    scale_two = lax.rsqrt(jnp.mean(residual * residual, -1, keepdims=True) + EPSILON)
    normed_two = (residual * scale_two * gain_two).astype(jnp.bfloat16)
    gate_up_full, down_full = (
        lax.all_gather(w_gate_up, ("dp", "ctx"), axis=0, tiled=True),
        lax.all_gather(w_down, ("dp", "ctx"), axis=0, tiled=True),
    )
    gate_up = full_product(normed_two, gate_up_full)
    gate_part = gate_up[:, :FF]
    up_part = gate_up[:, FF:]
    sigmoid = jax.nn.sigmoid(gate_part)
    hidden = (gate_part * sigmoid * up_part).astype(jnp.bfloat16)
    mlp_term = full_product(hidden, down_full)
    result = (residual + mlp_term).astype(jnp.bfloat16)
    gate_up_full, down_full = (
        lax.all_gather(w_gate_up, ("dp", "ctx"), axis=0, tiled=True),
        lax.all_gather(w_down, ("dp", "ctx"), axis=0, tiled=True),
    )
    grad_hidden = full_back(cotangent, down_full)
    grad_down = jnp.dot(cotangent.T, hidden, preferred_element_type=jnp.float32)
    grad_gate = grad_hidden * up_part * sigmoid * (1.0 + gate_part * (1.0 - sigmoid))
    grad_upper = grad_hidden * gate_part * sigmoid
    grad_gu = jnp.concatenate([grad_gate, grad_upper], 1).astype(jnp.bfloat16)
    grad_normed_two = full_back(grad_gu, gate_up_full)
    grad_w_gate_up = jnp.dot(grad_gu.T, normed_two, preferred_element_type=jnp.float32)
    grad_gain_two = jnp.sum(grad_normed_two * residual * scale_two, 0)
    mlp_owned = owned_three(grad_gain_two, grad_w_gate_up, grad_down)
    grad_residual = cotangent.astype(jnp.float32) + norm_back(
        grad_normed_two, gain_two, residual, scale_two
    )
    grad_res_bf = grad_residual.astype(jnp.bfloat16)
    qkv_full, out_full = (
        lax.all_gather(w_qkv, ("dp", "ctx"), axis=0, tiled=True),
        lax.all_gather(w_out, ("dp", "ctx"), axis=0, tiled=True),
    )
    attention_gradient = full_back(grad_res_bf, out_full).astype(jnp.bfloat16)
    grad_w_out = jnp.dot(grad_res_bf.T, attention_output, preferred_element_type=jnp.float32)
    keys_values_all = lax.all_gather(key_value, "ctx", axis=0, tiled=True)
    grouped_gradient = attention_gradient.reshape(
        count_of_rows, KEY_VALUE_HEADS, heads_ratio, HEAD_SIZE
    )
    attention_grouped = attention_output.reshape(
        count_of_rows, KEY_VALUE_HEADS, heads_ratio, HEAD_SIZE
    )
    row_delta = jnp.transpose(
        jnp.sum(grouped_gradient.astype(jnp.float32) * attention_grouped.astype(jnp.float32), -1),
        (1, 2, 0),
    )
    grouped_rows = keys_values_all.shape[0]
    block_rows = min(512, grouped_rows)
    block_count = grouped_rows // block_rows

    def key_block(grad_queries, which_block):
        start_row = which_block * block_rows
        block_portion = lax.dynamic_slice_in_dim(keys_values_all, start_row, block_rows, 0)
        scores, allowed, key_portion, value_portion = masked(block_portion, start_row)
        weights = jnp.where(allowed, jnp.exp(scores - log_total[..., None]), 0.0)
        grad_values = jnp.einsum(
            "gjrn,rgjd->ngd",
            weights.astype(jnp.bfloat16),
            grouped_gradient,
            preferred_element_type=jnp.float32,
        )
        grad_weights = jnp.einsum(
            "rgjd,ngd->gjrn", grouped_gradient, value_portion, preferred_element_type=jnp.float32
        )
        grad_scores = (weights * (grad_weights - row_delta[..., None])).astype(jnp.bfloat16)
        grad_queries = (
            grad_queries
            + jnp.einsum(
                "gjrn,ngd->rgjd", grad_scores, key_portion, preferred_element_type=jnp.float32
            )
            * score_scale
        )
        grad_keys = (
            jnp.einsum(
                "gjrn,rgjd->ngd", grad_scores, grouped_queries, preferred_element_type=jnp.float32
            )
            * score_scale
        )
        return (
            grad_queries,
            jnp.concatenate(
                [
                    grad_keys.reshape(block_rows, KEY_FEATURES),
                    grad_values.reshape(block_rows, KEY_FEATURES),
                ],
                1,
            ),
        )

    grad_queries, key_terms = lax.scan(
        key_block,
        jnp.zeros((count_of_rows, KEY_VALUE_HEADS, heads_ratio, HEAD_SIZE), jnp.float32),
        jnp.arange(block_count, dtype=jnp.int32),
    )
    key_value_gradient = lax.psum_scatter(
        key_terms.reshape(grouped_rows, 2 * KEY_FEATURES).astype(jnp.bfloat16),
        "ctx",
        scatter_dimension=0,
        tiled=True,
    ).astype(jnp.float32)
    grad_queries = rotate_back(
        grad_queries.reshape(count_of_rows, QUERY_HEADS, HEAD_SIZE), cosine_table, sine_values
    ).reshape(count_of_rows, QUERY_FEATURES)
    grad_keys = rotate_back(
        key_value_gradient[:, :KEY_FEATURES].reshape(count_of_rows, KEY_VALUE_HEADS, HEAD_SIZE),
        cosine_table,
        sine_values,
    ).reshape(count_of_rows, KEY_FEATURES)
    grad_projected = jnp.concatenate(
        [grad_queries, grad_keys, key_value_gradient[:, KEY_FEATURES:]], 1
    ).astype(jnp.bfloat16)
    grad_normed_one = full_back(grad_projected, qkv_full)
    grad_w_qkv = jnp.dot(grad_projected.T, normed_one, preferred_element_type=jnp.float32)
    grad_gain_one = jnp.sum(grad_normed_one * source * scale_one, 0)
    grad_tokens = grad_residual + norm_back(grad_normed_one, gain_one, source, scale_one)
    attn_owned = owned_three(grad_gain_one, grad_w_qkv, grad_w_out)
    return (
        result,
        grad_tokens,
        attn_owned[0],
        attn_owned[1],
        attn_owned[2],
        mlp_owned[0],
        mlp_owned[1],
        mlp_owned[2],
    )


def solution(mesh):
    return jax.shard_map(
        shards,
        mesh=mesh,
        in_specs=(
            P(("dp", "ctx"), None),
            P(("dp", "ctx")),
            P(("dp", "ctx"), None),
            P(("dp", "ctx"), None),
            P(("dp", "ctx")),
            P(("dp", "ctx"), None),
            P(("dp", "ctx"), None),
            P(("dp", "ctx"), None),
            P("dp", None),
            P("dp", None),
        ),
        out_specs=(
            P(("dp", "ctx"), None),
            P(("dp", "ctx"), None),
            P(("dp", "ctx")),
            P(("dp", "ctx"), None),
            P(("dp", "ctx"), None),
            P(("dp", "ctx")),
            P(("dp", "ctx"), None),
            P(("dp", "ctx"), None),
        ),
        check_vma=False,
    )
```

profile of v0, /device:TPU:0, one launch (start us, length us, event | category | flops | bytes accessed | tf_op | source)
XLA Modules:
  0.0 1631.1 jit_solution(5330102366979640390)
XLA Ops:
  8.0 0.9 dynamic-update-slice
  8.8 0.9 dynamic-update-slice.1
  9.7 0.8 reduce-window.9
  10.5 43.5 %all-reduce.5 = (f32[1536]{0:T(1024)S(1)}, f32[1536]{0:T(1024)S(1)}) all-reduce(f32[1536]{0:T(1024)S(1)} %dynamic-update-slice, f32[1536]{0:T(1024)S(1)} %dynamic-update-slice.1), channel_id=1, replica_groups=mesh['dp'=8,'ctx'=4] {'dp','ctx'}, use_global_device_ids=true, to_apply=%add | all-reduce | flops 3072 | bytes 24576
  54.9 1.4 fusion.26
  57.1 38.7 %all-gather.6.cloned.1.call-done = bf16[3072,1536]{1,0:T(8,128)(2,1)} async-done(((bf16[96,1536]{1,0:T(8,128)(2,1)}), bf16[3072,1536]{1,0:T(8,128)(2,1)}) %all-gather.6.cloned.1.call-update) | async-done | bytes 9437200 | tf_op jit(solution)/shard_map/all_gather | solution.py:105
  95.9 5.5 fusion.44
  101.4 1.7 copy-done.12
  103.7 0.9 pad_maximum_fusion.4
  107.9 1.6 slice.91
  110.2 1.1 pad_maximum_fusion.5
  111.3 20.5 %all-gather.8.cloned.1.call-done = bf16[1024,1536]{1,0:T(8,128)(2,1)} async-done(((bf16[256,1536]{1,0:T(8,128)(2,1)}), bf16[1024,1536]{1,0:T(8,128)(2,1)}) %all-gather.8.cloned.1.call-update) | async-done | bytes 3145744 | tf_op jit(solution)/shard_map/all_gather | solution.py:150
  131.9 2.1 fusion.69
  134.0 1.6 copy.64
  135.6 0.7 copy.65
  136.4 4.3 fusion.17
  140.7 4.0 fusion.18
  144.8 4.1 fusion.35
  148.9 49.5 %all-gather.10.cloned.1.call-done = bf16[1536,1536]{1,0:T(8,128)(2,1)} async-done(((bf16[48,1536]{1,0:T(8,128)(2,1)}), bf16[1536,1536]{1,0:T(8,128)(2,1)}) %all-gather.10.cloned.1.call-update) | async-done | bytes 4718608 | tf_op jit(solution)/shard_map/all_gather | solution.py:106
  198.4 3.9 multiply_reduce_fusion.3
  202.3 151.2 %all-gather.12.cloned.1.call-done = bf16[8192,1536]{1,0:T(8,128)(2,1)} async-done(((bf16[256,1536]{1,0:T(8,128)(2,1)}), bf16[8192,1536]{1,0:T(8,128)(2,1)}) %all-gather.12.cloned.1.call-update) | async-done | bytes 25165840 | tf_op jit(solution)/shard_map/all_gather | solution.py:173
  353.5 13.7 fusion.66
  367.2 82.5 %all-gather.14.cloned.1.call-done = bf16[1536,4096]{1,0:T(8,128)(2,1)} async-done(((bf16[48,4096]{1,0:T(8,128)(2,1)}), bf16[1536,4096]{1,0:T(8,128)(2,1)}) %all-gather.14.cloned.1.call-update) | async-done | bytes 12582928 | tf_op jit(solution)/shard_map/all_gather | solution.py:174
  449.6 13.2 multiply_convert_fusion.1
  462.9 13.9 multiply_reduce_fusion
  477.2 1.1 copy-done.2
  478.4 1.4 convolution_convert_fusion
  479.8 1.2 copy.68
  480.9 1.4 multiply_reduce_fusion.1
  482.3 59.7 %while.15 = (s32[]{:T(128)}, f32[256,8,2,96]{0,3,2,1:T(8,128)}, bf16[2,512,1536]{2,1,0:T(8,128)(2,1)}, s32[2]{0:T(128)S(1)}, bf16[1024,1536]{1,0:T(8,128)(2,1)},...) while((s32[]{:T(128)}, f32[256,8,2,96]{0,3,2,1:T(8,128)}, ...), condition=%wide.region_16.17_spmd.clone, body=%wide.region_13.16_spmd.clone.sunk | while | flops 2043966464 | bytes 114495864 | solution.py:260
  483.8 1.5 fusion.123
  485.5 5.7 fusion.124
  491.9 6.7 fusion.127
  498.6 4.3 bitcast_add_fusion.2
  502.9 0.9 copy-done.1
  503.8 3.6 fusion.128
  507.4 2.5 bitcast_multiply_fusion.2
  510.8 1.3 constant_dynamic-update-slice_fusion.2
  513.3 1.5 fusion.123
  515.0 5.7 fusion.124
  521.4 6.7 fusion.127
  528.1 4.8 bitcast_add_fusion.2
  532.9 0.9 copy-done.1
  533.8 3.6 fusion.128
  537.4 2.5 bitcast_multiply_fusion.2
  540.7 1.3 constant_dynamic-update-slice_fusion.2
  542.0 4.6 copy.71
  546.8 1.3 copy-done.3
  548.3 6.0 fusion.40
  555.1 1.6 add_convert_fusion
  556.9 26.3 %reduce-scatter.8.cloned.1.call-done = bf16[256,1536]{0,1:T(8,128)(2,1)} async-done(((bf16[1024,1536]{0,1:T(8,128)(2,1)}), bf16[256,1536]{0,1:T(8,128)(2,1)}) %reduce-scatter.8.cloned.1.call-update) | async-done | bytes 786448 | tf_op jit(solution)/shard_map/reduce_scatter | solution.py:265
  583.2 1.2 fusion.70
  585.1 9.6 fusion.38
  594.7 14.9 convolution_bitcast_fusion
  609.6 25.3 %copy.83 = f32[1536,4096]{1,0:T(8,128)} copy(f32[1536,4096]{0,1:T(8,128)} %convolution_bitcast_fusion) | data formatting | bytes 50331648
  635.6 22.7 %fusion.23 = f32[8192,1536]{1,0:T(8,128)} fusion(bf16[256,4096]{1,0:T(8,128)(2,1)} %copy-done.14, bf16[256,4096]{1,0:T(8,128)(2,1)} %copy-done.13, f32[256,1536]{1,0:T(8,128)} %copy-done.6, f32[1536]{0:T(1024)S(1)} %copy-done.25, f32[256]{0:T(256)} %copy-done.30), kind=kOutput, calls=%fused_computation.54 | convolution fusion | flops 6452019200 | bytes 56105984 | tf_op jit(solution)/shard_map/dot_general | solution.py:193
  658.4 10.2 fusion.25
  668.6 8.5 fusion.34
  677.1 41.0 %all-reduce.4 = (f32[1536]{0:T(1024)S(1)}, f32[1536]{0:T(1024)S(1)}) all-reduce(f32[1536]{0:T(1024)} %get-tuple-element.305, f32[1536]{0:T(1024)} %get-tuple-element.303), channel_id=3, replica_groups=mesh['dp'=8,'ctx'=4] {'dp','ctx'}, use_global_device_ids=true, to_apply=%region_20.21.clone | all-reduce | flops 3072 | bytes 24576
  719.9 3.0 fusion.31
  722.9 3.4 reduce-scatter.12.cloned.1.call-done
  726.3 212.8 %reduce-scatter.10.cloned.1.call-done = f32[96,1536]{1,0:T(8,128)} async-done(((f32[3072,1536]{1,0:T(8,128)}), f32[96,1536]{1,0:T(8,128)}) %reduce-scatter.10.cloned.1.call-update) | async-done | bytes 589840 | tf_op jit(solution)/shard_map/reduce_scatter | solution.py:82
  939.1 249.2 %reduce-scatter.16.cloned.1.call-done = f32[48,4096]{1,0:T(8,128)} async-done(((f32[1536,4096]{1,0:T(8,128)}), f32[48,4096]{1,0:T(8,128)}) %reduce-scatter.16.cloned.1.call-update) | async-done | bytes 786448
  1188.3 435.5 %reduce-scatter.14.cloned.1.call-done = f32[256,1536]{1,0:T(8,128)} async-done(((f32[8192,1536]{1,0:T(8,128)}), f32[256,1536]{1,0:T(8,128)}) %reduce-scatter.14.cloned.1.call-update) | async-done | bytes 1572880 | tf_op jit(solution)/shard_map/reduce_scatter | solution.py:82
  (149 shorter events, 16.7 us)
Async XLA Ops:
  7.2 88.7 %all-gather.6.cloned.1.call-start = ((), (), s32[]{:S(2)}) async-start(), calls=%async_computation.5 | async-start | bytes 9732096 | tf_op jit(solution)/shard_map/all_gather | solution.py:105
  7.9 124.0 %all-gather.8.cloned.1.call-start = ((), (), s32[]{:S(2)}) async-start(), calls=%async_computation.6 | async-start | bytes 3932160 | tf_op jit(solution)/shard_map/all_gather | solution.py:150
  54.0 47.3 %copy-start.22 = (f32[1536]{0:T(1024)}, f32[1536]{0:T(1024)S(1)}, u32[]{:S(2)}) copy-start(f32[1536]{0:T(1024)S(1)} %get-tuple-element.337) | copy-start | bytes 18436
  54.0 422.7 %copy-start.24 = (f32[1536]{0:T(1024)}, f32[1536]{0:T(1024)S(1)}, u32[]{:S(2)}) copy-start(f32[1536]{0:T(1024)S(1)} %get-tuple-element.338) | copy-start | bytes 18436
  56.8 44.5 %copy-start.27 = (f32[256]{0:T(256)}, f32[256]{0:T(256)S(1)}, u32[]{:S(2)}) copy-start(f32[256]{0:T(256)S(1)} %get-tuple-element.359) | copy-start | bytes 3076
  57.1 52.8 %copy-start.18 = (f32[256,48]{0,1:T(8,128)}, f32[256,48]{0,1:T(8,128)S(1)}, u32[]{:S(2)}) copy-start(f32[256,48]{0,1:T(8,128)S(1)} %get-tuple-element.356) | copy-start | bytes 147460
  57.1 52.8 %copy-start.20 = (f32[256,48]{0,1:T(8,128)}, f32[256,48]{0,1:T(8,128)S(1)}, u32[]{:S(2)}) copy-start(f32[256,48]{0,1:T(8,128)S(1)} %get-tuple-element.357) | copy-start | bytes 147460
  101.3 1.7 copy-start.12
  103.5 3.7 copy-start.32
  103.5 3.8 copy-start.26
  104.7 93.7 %all-gather.10.cloned.1.call-start = ((), (), s32[]{:S(2)}) async-start(), calls=%async_computation.7 | async-start | bytes 4866048 | tf_op jit(solution)/shard_map/all_gather | solution.py:106
  105.4 248.1 %all-gather.12.cloned.1.call-start = ((), (), s32[]{:S(2)}) async-start(), calls=%async_computation.8 | async-start | bytes 25952256 | tf_op jit(solution)/shard_map/all_gather | solution.py:173
  106.0 343.6 %all-gather.14.cloned.1.call-start = ((), (), s32[]{:S(2)}) async-start(), calls=%async_computation.9 | async-start | bytes 12976128 | tf_op jit(solution)/shard_map/all_gather | solution.py:174
  106.6 476.6 %reduce-scatter.8.cloned.1.call-start = ((), (), s32[]{:S(2)}) async-start(), calls=%async_computation.10 | async-start | bytes 3932160 | tf_op jit(solution)/shard_map/reduce_scatter | solution.py:265
  110.2 1.1 copy-start.7
  110.2 1.1 copy-start.8
  140.7 4.1 copy-start.15
  144.8 53.6 %copy-start.4 = (bf16[256,1536]{1,0:T(8,128)(2,1)S(1)}, bf16[256,1536]{1,0:T(8,128)(2,1)}, u32[]{:S(2)}) copy-start(bf16[256,1536]{1,0:T(8,128)(2,1)} %param.12) | copy-start | bytes 2359300
  148.9 332.0 %copy-start.9 = (bf16[256,8,2,96]{0,3,2,1:T(8,128)(2,1)}, bf16[256,8,2,96]{0,3,2,1:T(8,128)(2,1)S(1)}, u32[]{:S(2)}) copy-start(bf16[256,8,2,96]{0,3,2,1:T(8,128)(2,1)S(1)} %fusion.35) | copy-start | bytes 2359300
  202.2 274.5 %copy-start.6 = (f32[256,1536]{1,0:T(8,128)}, f32[256,1536]{1,0:T(8,128)S(1)}, u32[]{:S(2)}) copy-start(f32[256,1536]{1,0:T(8,128)S(1)} %get-tuple-element.365) | copy-start | bytes 4718596
  202.3 274.5 %copy-start.30 = (f32[256]{0:T(256)}, f32[256]{0:T(256)S(1)}, u32[]{:S(2)}) copy-start(f32[256]{0:T(256)S(1)} %get-tuple-element.361) | copy-start | bytes 3076
  353.5 96.1 %copy-start.11 = (bf16[256,1536]{1,0:T(8,128)(2,1)S(1)}, bf16[256,1536]{1,0:T(8,128)(2,1)}, u32[]{:S(2)}) copy-start(bf16[256,1536]{1,0:T(8,128)(2,1)} %param.19) | copy-start | bytes 2359300
  449.6 28.7 %slice-start = ((s8[4718592]{0:T(1024)(128)(4,1)}), s8[4194304]{0:T(1024)(128)(4,1)S(1)}, s32[]{:S(2)}) async-start(s8[4718592]{0:T(1024)(128)(4,1)} %bitcast.195), calls=%async_computation.15 | async-start | bytes 8388608
  462.9 13.9 copy-start.13
  462.9 13.9 copy-start.14
  462.9 15.5 slice-start.1
  477.2 1.1 copy-start.2
  498.6 5.2 copy-start.1
  503.8 3.6 copy-start
  528.1 5.7 copy-start.1
  533.8 3.6 copy-start
  546.7 1.4 copy-start.3
  546.7 1.6 copy-start.10
  546.7 179.6 %reduce-scatter.12.cloned.1.call-start = ((), (), s32[]{:S(2)}) async-start(), calls=%async_computation.12 | async-start | bytes 9732096 | tf_op jit(solution)/shard_map/reduce_scatter | solution.py:83
  554.3 0.8 copy-start.19
  554.3 0.8 copy-start.21
  554.3 384.8 %reduce-scatter.10.cloned.1.call-start = ((), (), s32[]{:S(2)}) async-start(), calls=%async_computation.11 | async-start | bytes 19464192 | tf_op jit(solution)/shard_map/reduce_scatter | solution.py:82
  556.8 28.3 %copy-start.5 = (bf16[256,1536]{1,0:T(8,128)(2,1)S(1)}, bf16[256,1536]{1,0:T(8,128)(2,1)}, u32[]{:S(2)}) copy-start(bf16[256,1536]{1,0:T(8,128)(2,1)} %param.12) | copy-start | bytes 2359300
  556.8 28.2 %copy-start.23 = (f32[1536]{0:T(1024)S(1)}, f32[1536]{0:T(1024)}, u32[]{:S(2)}) copy-start(f32[1536]{0:T(1024)} %copy-done.22) | copy-start | bytes 18436
  556.9 28.2 %copy-start.28 = (f32[256]{0:T(256)S(1)}, f32[256]{0:T(256)}, u32[]{:S(2)}) copy-start(f32[256]{0:T(256)} %copy-done.27) | copy-start | bytes 3076
  584.3 0.8 copy-start.16
  594.7 593.6 %reduce-scatter.16.cloned.1.call-start = ((), (), s32[]{:S(2)}) async-start(), calls=%async_computation.14 | async-start | bytes 25952256
  634.9 0.7 copy-start.25
  635.0 988.9 %reduce-scatter.14.cloned.1.call-start = ((), (), s32[]{:S(2)}) async-start(), calls=%async_computation.13 | async-start | bytes 51904512 | tf_op jit(solution)/shard_map/reduce_scatter | solution.py:82
  658.4 10.2 copy-start.17
  658.4 10.2 copy-start.29
  668.6 51.4 %copy-start.31 = (f32[256]{0:T(256)S(1)}, f32[256]{0:T(256)}, u32[]{:S(2)}) copy-start(f32[256]{0:T(256)} %get-tuple-element.358) | copy-start | bytes 3076
Sparse Core Ops, SparseCore 0:
  10.9 84.9 all-gather.5
  104.8 27.0 all-gather.7
  134.8 63.5 all-gather.9
  201.1 152.3 all-gather.11
  356.2 93.3 all-gather.13
  546.8 36.2 reduce-scatter.7
  589.6 136.6 reduce-scatter.11
  733.3 205.7 reduce-scatter.9
  946.1 242.1 reduce-scatter.15
  1195.1 428.6 reduce-scatter.13
where the time goes:
time: 1640 us; the launch traced here: 1630 us
  waiting for transfers between devices  1270 us (77%)
  matrix products  178 us (11%)
  blocking collectives  84.6 us (5%)
  local copies, waits for them, and re-layouts  59.6 us (4%)
  other arithmetic  19.4 us (1%)
    reduce_scatter x2, waiting for transfers between devices, owned_three(): lax.psum_scatter(second_part, ('dp', 'ctx'), scatter_dimension=0, tiled=T...  648 us
    unnamed x11, waiting for transfers between devices  252 us
    all_gather x1, waiting for transfers between devices, shards(): lax.all_gather(w_gate_up, ('dp', 'ctx'), axis=0, tiled=True)  151 us
    unnamed x2, blocking collectives  84.6 us
    all_gather x1, waiting for transfers between devices, shards(): lax.all_gather(w_down, ('dp', 'ctx'), axis=0, tiled=True)  82.5 us
    all_gather x1, waiting for transfers between devices, shards(): lax.all_gather(w_out, ('dp', 'ctx'), axis=0, tiled=True)  49.5 us
    all_gather x1, waiting for transfers between devices, shards(): lax.all_gather(w_qkv, ('dp', 'ctx'), axis=0, tiled=True)  38.7 us
    dot_general x4, matrix products, full_back(): return jnp.dot(grad_side, whole_weight, preferred_element_type=jnp.float32)  37 us
  transfers between devices with their start and end apart: 10, of which 10 were waited for; matrix products, arithmetic and copies ran while one was open for 9% of the time, Pallas kernels for 0%

commit v1 on v0

--- a/solution.py
+++ b/solution.py
@@ -14,6 +14,18 @@
 EPSILON = 1e-05
 THETA = 100000.0
 MASK_FILL = -1e30
+
+
+def gather_by_bits(x, axis, dim):
+    ways, here, step = (lax.axis_size(axis), lax.axis_index(axis), x.shape[dim])
+    line, have = (x, 1)
+    while have < ways:
+        line = jnp.concatenate(
+            [line, lax.ppermute(line, axis, [(d, (d - have) % ways) for d in range(ways)])],
+            axis=dim,
+        )
+        have = 2 * have
+    return jnp.roll(line, here * step, axis=dim)
 
 
 def rope_tables(rope_pos):
@@ -170,7 +182,7 @@
     scale_two = lax.rsqrt(jnp.mean(residual * residual, -1, keepdims=True) + EPSILON)
     normed_two = (residual * scale_two * gain_two).astype(jnp.bfloat16)
     gate_up_full, down_full = (
-        lax.all_gather(w_gate_up, ("dp", "ctx"), axis=0, tiled=True),
+        gather_by_bits(w_gate_up, ("dp", "ctx"), 0),
         lax.all_gather(w_down, ("dp", "ctx"), axis=0, tiled=True),
     )
     gate_up = full_product(normed_two, gate_up_full)

time: 1640 us -> 2360 us (1.44)
  waiting for transfers between devices: 1270 us -> 1920 us
  local copies, waits for them, and re-layouts: 59.6 us -> 125 us
    ppermute x0 -> x5, waiting for transfers between devices: none -> 522 us  [gather_by_bits(): lax.ppermute(line, axis, [(d, (d - have) % ways) for d in range(ways)])]
    all_gather x1, waiting for transfers between devices: 49.5 us -> 261 us  [shards(): lax.all_gather(w_out, ('dp', 'ctx'), axis=0, tiled=True)]
    reduce_scatter x1, waiting for transfers between devices: 3.36 us -> 142 us  [owned_three(): lax.psum_scatter(third_part, ('dp', 'ctx'), scatter_dimension=0, tiled=True)]
    unnamed x11, waiting for transfers between devices: 252 us -> 135 us
    all_gather x1, waiting for transfers between devices: 82.5 us -> 26 us  [shards(): lax.all_gather(w_down, ('dp', 'ctx'), axis=0, tiled=True)]
    unnamed x73 -> x95, local copies, waits for them, and re-layouts: 34.6 us -> 64 us
    reduce_scatter x1, waiting for transfers between devices: 26.3 us -> 0.02 us  [shards(): lax.psum_scatter(key_terms.reshape(grouped_rows, 2 * KEY_FEATURES).astype...]
  transfers between devices with their start and end apart: 10 -> 15, of which waited for: 10 -> 13; matrix products, arithmetic and copies ran while one was open for 9% -> 9% of each run, Pallas kernels for 0% -> 0%
where the time goes in v1:
time: 2360 us; the launch traced here: 2350 us
  waiting for transfers between devices  1920 us (81%)
  matrix products  175 us (7%)
  local copies, waits for them, and re-layouts  125 us (5%)
  blocking collectives  85 us (4%)
    reduce_scatter x2, waiting for transfers between devices, owned_three(): lax.psum_scatter(second_part, ('dp', 'ctx'), scatter_dimension=0, tiled=T...  648 us
    ppermute x5, waiting for transfers between devices, gather_by_bits(): lax.ppermute(line, axis, [(d, (d - have) % ways) for d in range(ways)])  522 us
    all_gather x1, waiting for transfers between devices, shards(): lax.all_gather(w_out, ('dp', 'ctx'), axis=0, tiled=True)  261 us
    reduce_scatter x1, waiting for transfers between devices, owned_three(): lax.psum_scatter(third_part, ('dp', 'ctx'), scatter_dimension=0, tiled=True)  142 us
    all_gather x1, waiting for transfers between devices, shards(): lax.all_gather(w_gate_up, ('dp', 'ctx'), axis=0, tiled=True)  142 us
    unnamed x11, waiting for transfers between devices  135 us
    unnamed x2, blocking collectives  85 us
    unnamed x95, local copies, waits for them, and re-layouts  64 us
  transfers between devices with their start and end apart: 15, of which 13 were waited for; matrix products, arithmetic and copies ran while one was open for 9% of the time, Pallas kernels for 0%

profile of v1, /device:TPU:0, one launch (start us, length us, event | category | flops | bytes accessed | tf_op | source)
XLA Modules:
  0.0 2354.0 jit_solution(6308428788389417193)
XLA Ops:
  10.5 42.7 %all-reduce.5 = (f32[1536]{0:T(1024)S(1)}, f32[1536]{0:T(1024)S(1)}) all-reduce(f32[1536]{0:T(1024)S(1)} %dynamic-update-slice, f32[1536]{0:T(1024)S(1)} %dynamic-update-slice.1), channel_id=1, replica_groups=mesh['dp'=8,'ctx'=4] {'dp','ctx'}, use_global_device_ids=true, to_apply=%add | all-reduce | flops 3072 | bytes 24576
  56.2 39.8 %all-gather.6.cloned.1.call-done = bf16[3072,1536]{1,0:T(8,128)(2,1)} async-done(((bf16[96,1536]{1,0:T(8,128)(2,1)}), bf16[3072,1536]{1,0:T(8,128)(2,1)}) %all-gather.6.cloned.1.call-update) | async-done | bytes 9437200 | tf_op jit(solution)/shard_map/all_gather | solution.py:117
  96.1 5.5 fusion.46
  101.6 1.6 copy-done.21
  106.8 2.7 collective-permute-start
  109.4 9.5 collective-permute-done
  119.0 8.5 collective-permute-start.1
  127.5 41.2 %collective-permute-done.1 = bf16[512,1536]{1,0:T(8,128)(2,1)S(1)} collective-permute-done((bf16[512,1536]{1,0:T(8,128)(2,1)S(1)}, bf16[512,1536]{1,0:T(8,128)(2,1)S(1)}, u32[]{:S(2)}, u32[]{:S(2)}) %collective-permute-start.1) | collective-permute-done | bytes 1572896 | tf_op jit(solution)/shard_map/ppermute | solution.py:24
  168.9 2.8 collective-permute-start.2
  171.7 71.0 %collective-permute-done.2 = bf16[1024,1536]{1,0:T(8,128)(2,1)S(1)} collective-permute-done((bf16[1024,1536]{1,0:T(8,128)(2,1)S(1)}, bf16[1024,1536]{1,0:T(8,128)(2,1)S(1)}, u32[]{:S(2)}, u32[]{:S(2)}) %collective-permute-start.2) | collective-permute-done | bytes 3145760 | tf_op jit(solution)/shard_map/ppermute | solution.py:24
  248.0 2.1 constant_dynamic-update-slice_fusion.2
  250.1 136.4 %collective-permute-done.3 = bf16[2048,1536]{1,0:T(8,128)(2,1)} collective-permute-done((bf16[2048,1536]{1,0:T(8,128)(2,1)S(1)}, bf16[2048,1536]{1,0:T(8,128)(2,1)}, u32[]{:S(2)}, u32[]{:S(2)}) %collective-permute-start.3) | collective-permute-done | bytes 6291488 | tf_op jit(solution)/shard_map/ppermute | solution.py:24
  386.6 8.2 constant_dynamic-update-slice_fusion.1
  396.5 2.7 slice.91
  399.1 3.0 copy.66
  402.1 1.6 subtract_convert_fusion.1
  404.7 3.8 fusion.71
  408.5 2.8 copy.65
  411.3 2.6 copy.64
  413.8 4.3 fusion.19
  418.2 4.0 fusion.20
  422.2 4.9 fusion.37
  427.1 261.1 %all-gather.10.cloned.1.call-done = bf16[1536,1536]{1,0:T(8,128)(2,1)} async-done(((bf16[48,1536]{1,0:T(8,128)(2,1)}), bf16[1536,1536]{1,0:T(8,128)(2,1)}) %all-gather.10.cloned.1.call-update) | async-done | bytes 4718608 | tf_op jit(solution)/shard_map/all_gather | solution.py:118
  688.2 5.4 multiply_reduce_fusion.3
  693.6 264.0 %collective-permute-done.4 = bf16[4096,1536]{1,0:T(8,128)(2,1)} collective-permute-done((bf16[4096,1536]{1,0:T(8,128)(2,1)}, bf16[4096,1536]{1,0:T(8,128)(2,1)}, u32[]{:S(2)}, u32[]{:S(2)}) %collective-permute-start.4) | collective-permute-done | bytes 12582944 | tf_op jit(solution)/shard_map/ppermute | solution.py:24
  957.6 10.6 constant_dynamic-update-slice_fusion.12
  971.5 1.9 constant_dynamic-update-slice_fusion.8
  973.4 5.9 constant_dynamic-update-slice_fusion.7
  979.3 10.6 constant_dynamic-update-slice_fusion.6
  990.0 14.9 fusion.17
  1004.8 26.0 %all-gather.12.cloned.1.call-done = bf16[1536,4096]{1,0:T(8,128)(2,1)} async-done(((bf16[48,4096]{1,0:T(8,128)(2,1)}), bf16[1536,4096]{1,0:T(8,128)(2,1)}) %all-gather.12.cloned.1.call-update) | async-done | bytes 12582928 | tf_op jit(solution)/shard_map/all_gather | solution.py:186
  1030.8 13.7 multiply_convert_fusion.1
  1044.5 141.7 %all-gather.14.cloned.1.call-done = bf16[8192,1536]{1,0:T(8,128)(2,1)} async-done(((bf16[256,1536]{1,0:T(8,128)(2,1)}), bf16[8192,1536]{1,0:T(8,128)(2,1)}) %all-gather.14.cloned.1.call-update) | async-done | bytes 25165840 | tf_op jit(solution)/shard_map/all_gather | solution.py:196
  1186.2 13.7 multiply_reduce_fusion
  1205.4 59.4 %while.15 = (s32[]{:T(128)}, f32[256,8,2,96]{0,3,2,1:T(8,128)}, bf16[2,512,1536]{2,1,0:T(8,128)(2,1)}, s32[2]{0:T(128)S(1)}, bf16[1024,1536]{1,0:T(8,128)(2,1)},...) while((s32[]{:T(128)}, f32[256,8,2,96]{0,3,2,1:T(8,128)}, ...), condition=%wide.region_16.17_spmd.clone, body=%wide.region_13.16_spmd.clone.sunk | while | flops 2043966464 | bytes 127079328 | solution.py:272
  1209.3 4.6 fusion.125
  1214.2 5.5 fusion.128
  1219.7 1.9 copy-done
  1223.1 3.4 fusion.129
  1226.7 1.6 copy.103
  1228.2 2.8 constant_dynamic-update-slice_fusion.19
  1231.0 3.1 bitcast_add_fusion.2
  1238.7 4.6 fusion.125
  1243.6 5.5 fusion.128
  1249.2 1.9 copy-done
  1252.6 3.4 fusion.129
  1256.1 1.6 copy.103
  1257.7 2.8 constant_dynamic-update-slice_fusion.19
  1260.5 3.1 bitcast_add_fusion.2
  1264.8 4.6 copy.71
  1269.5 1.5 copy-done.14
  1271.2 10.9 convolution_bitcast_fusion
  1282.1 24.8 %copy.83 = f32[1536,4096]{1,0:T(8,128)} copy(f32[1536,4096]{0,1:T(8,128)} %convolution_bitcast_fusion) | data formatting | bytes 50331648
  1308.5 5.0 fusion.42
  1317.3 11.1 fusion.40
  1329.1 28.4 %fusion.25 = f32[8192,1536]{1,0:T(8,128)} fusion(bf16[256,4096]{1,0:T(8,128)(2,1)} %get-tuple-element.342, bf16[256,4096]{1,0:T(8,128)(2,1)} %get-tuple-element.341, f32[256,1536]{1,0:T(8,128)} %get-tuple-element.375, f32[1536]{0:T(1024)S(1)} %copy-done.33, f32[256]{0:T(256)} %copy-done.38), kind=kOutput, calls=%fused_computation.58 | convolution fusion | flops 6452019200 | bytes 56105984 | tf_op jit(solution)/shard_map/dot_general | solution.py:205
  1357.5 11.6 fusion.27
  1369.1 8.2 fusion.36
  1377.3 42.3 %all-reduce.4 = (f32[1536]{0:T(1024)S(1)}, f32[1536]{0:T(1024)S(1)}) all-reduce(f32[1536]{0:T(1024)} %get-tuple-element.305, f32[1536]{0:T(1024)} %get-tuple-element.303), channel_id=3, replica_groups=mesh['dp'=8,'ctx'=4] {'dp','ctx'}, use_global_device_ids=true, to_apply=%region_20.21.clone | all-reduce | flops 3072 | bytes 24576
  1421.4 3.0 fusion.33
  1424.4 132.3 %reduce-scatter.16.cloned.1.call-done = f32[48,4096]{1,0:T(8,128)} async-done(((f32[1536,4096]{1,0:T(8,128)}), f32[48,4096]{1,0:T(8,128)}) %reduce-scatter.16.cloned.1.call-update) | async-done | bytes 786448
  1556.7 142.2 %reduce-scatter.12.cloned.1.call-done = f32[48,1536]{1,0:T(8,128)} async-done(((f32[1536,1536]{1,0:T(8,128)}), f32[48,1536]{1,0:T(8,128)}) %reduce-scatter.12.cloned.1.call-update) | async-done | bytes 294928 | tf_op jit(solution)/shard_map/reduce_scatter | solution.py:95
  1698.9 212.8 %reduce-scatter.10.cloned.1.call-done = f32[96,1536]{1,0:T(8,128)} async-done(((f32[3072,1536]{1,0:T(8,128)}), f32[96,1536]{1,0:T(8,128)}) %reduce-scatter.10.cloned.1.call-update) | async-done | bytes 589840 | tf_op jit(solution)/shard_map/reduce_scatter | solution.py:94
  1911.7 435.2 %reduce-scatter.14.cloned.1.call-done = f32[256,1536]{1,0:T(8,128)} async-done(((f32[8192,1536]{1,0:T(8,128)}), f32[256,1536]{1,0:T(8,128)}) %reduce-scatter.14.cloned.1.call-update) | async-done | bytes 1572880 | tf_op jit(solution)/shard_map/reduce_scatter | solution.py:94
  (194 shorter events, 46.3 us)
Async XLA Ops:
  7.2 88.9 %all-gather.6.cloned.1.call-start = ((), (), s32[]{:S(2)}) async-start(), calls=%async_computation.5 | async-start | bytes 9732096 | tf_op jit(solution)/shard_map/all_gather | solution.py:117
  7.9 396.8 %all-gather.8.cloned.1.call-start = ((), (), s32[]{:S(2)}) async-start(), calls=%async_computation.6 | async-start | bytes 3932160 | tf_op jit(solution)/shard_map/all_gather | solution.py:162
  53.2 48.4 %copy-start.30 = (f32[1536]{0:T(1024)}, f32[1536]{0:T(1024)S(1)}, u32[]{:S(2)}) copy-start(f32[1536]{0:T(1024)S(1)} %get-tuple-element.337) | copy-start | bytes 18436
  53.2 1146.7 %copy-start.32 = (f32[1536]{0:T(1024)}, f32[1536]{0:T(1024)S(1)}, u32[]{:S(2)}) copy-start(f32[1536]{0:T(1024)S(1)} %get-tuple-element.338) | copy-start | bytes 18436
  56.0 45.6 %copy-start.35 = (f32[256]{0:T(256)}, f32[256]{0:T(256)S(1)}, u32[]{:S(2)}) copy-start(f32[256]{0:T(256)S(1)} %get-tuple-element.369) | copy-start | bytes 3076
  56.2 345.9 %copy-start.25 = (f32[256,48]{0,1:T(8,128)}, f32[256,48]{0,1:T(8,128)S(1)}, u32[]{:S(2)}) copy-start(f32[256,48]{0,1:T(8,128)S(1)} %get-tuple-element.366) | copy-start | bytes 147460
  56.2 345.9 %copy-start.27 = (f32[256,48]{0,1:T(8,128)}, f32[256,48]{0,1:T(8,128)S(1)}, u32[]{:S(2)}) copy-start(f32[256,48]{0,1:T(8,128)S(1)} %get-tuple-element.367) | copy-start | bytes 147460
  101.6 1.6 copy-start.21
  103.5 3.2 copy-start.5
  104.8 583.4 %all-gather.10.cloned.1.call-start = ((), (), s32[]{:S(2)}) async-start(), calls=%async_computation.7 | async-start | bytes 4866048 | tf_op jit(solution)/shard_map/all_gather | solution.py:118
  105.5 925.3 %all-gather.12.cloned.1.call-start = ((), (), s32[]{:S(2)}) async-start(), calls=%async_computation.8 | async-start | bytes 12976128 | tf_op jit(solution)/shard_map/all_gather | solution.py:186
  106.1 1080.1 %all-gather.14.cloned.1.call-start = ((), (), s32[]{:S(2)}) async-start(), calls=%async_computation.9 | async-start | bytes 25952256 | tf_op jit(solution)/shard_map/all_gather | solution.py:196
  106.7 1208.6 %reduce-scatter.8.cloned.1.call-start = ((), (), s32[]{:S(2)}) async-start(), calls=%async_computation.10 | async-start | bytes 3932160 | tf_op jit(solution)/shard_map/reduce_scatter | solution.py:277
  106.8 12.2 collective-permute-start
  118.9 126.7 %copy-start.8 = (bf16[256,1536]{1,0:T(8,128)(2,1)}, bf16[256,1536]{1,0:T(8,128)(2,1)S(1)}, u32[]{:S(2)}) copy-start(bf16[256,1536]{1,0:T(8,128)(2,1)S(1)} %collective-permute-done) | copy-start | bytes 2359300
  119.0 49.6 %collective-permute-start.1 = (bf16[512,1536]{1,0:T(8,128)(2,1)S(1)}, bf16[512,1536]{1,0:T(8,128)(2,1)S(1)}, u32[]{:S(2)}, u32[]{:S(2)}) collective-permute-start(bf16[512,1536]{1,0:T(8,128)(2,1)S(1)} %pad_maximum_fusion.5), channel_id=1, source_target_pairs={{0,30},{1,31},{2,0},{3,1},{4,2},{5,3},{6,4},{7,5},{8,6},{9,7},{10,... | collective-permute-start | bytes 4718600 | tf_op jit(solution)/shard_map/ppermute | solution.py:24
  168.9 73.8 %collective-permute-start.2 = (bf16[1024,1536]{1,0:T(8,128)(2,1)S(1)}, bf16[1024,1536]{1,0:T(8,128)(2,1)S(1)}, u32[]{:S(2)}, u32[]{:S(2)}) collective-permute-start(bf16[1024,1536]{1,0:T(8,128)(2,1)S(1)} %pad_maximum_fusion.2), channel_id=1, source_target_pairs={{0,28},{1,29},{2,30},{3,31},{4,0},{5,1},{6,2},{7,3},{8,4},{9,5},{1... | collective-permute-start | bytes 9437192 | tf_op jit(solution)/shard_map/ppermute | solution.py:24
  242.7 5.3 copy-start.6
  243.2 143.4 %collective-permute-start.3 = (bf16[2048,1536]{1,0:T(8,128)(2,1)S(1)}, bf16[2048,1536]{1,0:T(8,128)(2,1)}, u32[]{:S(2)}, u32[]{:S(2)}) collective-permute-start(bf16[2048,1536]{1,0:T(8,128)(2,1)S(1)} %pad_maximum_fusion), channel_id=1, source_target_pairs={{0,24},{1,25},{2,26},{3,27},{4,28},{5,29},{6,30},{7,31},{8,0},{9,1... | collective-permute-start | bytes 18874376 | tf_op jit(solution)/shard_map/ppermute | solution.py:24
  250.1 136.4 %copy-start.29 = (bf16[4096,1536]{1,0:T(8,128)(2,1)}, bf16[4096,1536]{1,0:T(8,128)(2,1)S(1)}, u32[]{:S(2)}) copy-start(bf16[4096,1536]{1,0:T(8,128)(2,1)S(1)} %get-tuple-element.346) | copy-start | bytes 37748740
  386.6 9.2 copy-start.40
  386.6 9.4 copy-start.34
  394.8 562.9 %collective-permute-start.4 = (bf16[4096,1536]{1,0:T(8,128)(2,1)}, bf16[4096,1536]{1,0:T(8,128)(2,1)}, u32[]{:S(2)}, u32[]{:S(2)}) collective-permute-start(bf16[4096,1536]{1,0:T(8,128)(2,1)} %get-tuple-element.344), channel_id=1, source_target_pairs={{0,16},{1,17},{2,18},{3,19},{4,20},{5,21},{6,22},{7,23},{8,24},{9,... | collective-permute-start | bytes 37748744 | tf_op jit(solution)/shard_map/ppermute | solution.py:24
  403.7 0.7 copy-start.15
  403.7 0.9 copy-start.16
  418.2 4.1 copy-start.22
  693.6 506.3 %copy-start.38 = (f32[256]{0:T(256)}, f32[256]{0:T(256)S(1)}, u32[]{:S(2)}) copy-start(f32[256]{0:T(256)S(1)} %get-tuple-element.371) | copy-start | bytes 3076
  957.6 11.7 copy-start.9
  968.3 3.2 copy-start.7
  979.3 10.6 copy-start.13
  990.0 40.9 %copy-start.19 = (bf16[256,1536]{1,0:T(8,128)(2,1)S(1)}, bf16[256,1536]{1,0:T(8,128)(2,1)}, u32[]{:S(2)}) copy-start(bf16[256,1536]{1,0:T(8,128)(2,1)} %param.19) | copy-start | bytes 2359300
  1186.2 15.3 slice-start
  1186.2 15.3 slice-start.1
  1200.3 1.1 copy-start.10
  1201.5 2.5 copy-start.17
  1214.2 8.9 copy-start.1
  1219.7 2.0 copy-start
  1228.2 2.8 copy-start.2
  1234.1 1.2 copy-start.3
  1243.6 8.9 copy-start.1
  1249.2 2.0 copy-start
  1257.7 2.8 copy-start.2
  1263.6 1.2 copy-start.3
  1269.4 1.6 copy-start.14
  1269.4 1.8 copy-start.20
  1269.5 287.2 %reduce-scatter.16.cloned.1.call-start = ((), (), s32[]{:S(2)}) async-start(), calls=%async_computation.14 | async-start | bytes 25952256
  1306.9 1.4 copy-start.11
  1306.9 1.6 copy-start.18
  1306.9 392.0 %reduce-scatter.12.cloned.1.call-start = ((), (), s32[]{:S(2)}) async-start(), calls=%async_computation.12 | async-start | bytes 9732096 | tf_op jit(solution)/shard_map/reduce_scatter | solution.py:95
  1313.5 1.4 copy-start.4
  1313.5 1.4 copy-start.26
  1313.5 1.4 copy-start.28
  1313.5 598.2 %reduce-scatter.10.cloned.1.call-start = ((), (), s32[]{:S(2)}) async-start(), calls=%async_computation.11 | async-start | bytes 19464192 | tf_op jit(solution)/shard_map/reduce_scatter | solution.py:94
  1315.1 2.1 copy-start.12
  1315.1 2.1 copy-start.31
  1315.2 2.1 copy-start.36
  1316.5 0.8 copy-start.23
  1328.4 0.7 copy-start.33
  1328.4 1018.6 %reduce-scatter.14.cloned.1.call-start = ((), (), s32[]{:S(2)}) async-start(), calls=%async_computation.13 | async-start | bytes 51904512 | tf_op jit(solution)/shard_map/reduce_scatter | solution.py:94
  1357.4 11.6 copy-start.24
  1357.5 11.6 copy-start.37
  1369.1 52.3 %copy-start.39 = (f32[256]{0:T(256)S(1)}, f32[256]{0:T(256)}, u32[]{:S(2)}) copy-start(f32[256]{0:T(256)} %get-tuple-element.368) | copy-start | bytes 3076
Sparse Core Ops, SparseCore 0:
  10.9 85.1 all-gather.5
  104.9 64.2 all-gather.7
  172.2 516.0 all-gather.9
  691.0 339.8 all-gather.11
  1033.6 152.6 all-gather.13
  1269.6 35.8 reduce-scatter.7
  1312.5 244.1 reduce-scatter.15
  1563.2 135.7 reduce-scatter.11
  1705.9 205.7 reduce-scatter.9
  1918.6 428.3 reduce-scatter.13
